TPU v7x, 32 devices: a whole 2x2x4 slice. The times are simulated.
32 devices in a mesh: vocab: 16 (over z, x, core), seq: 2 (over y).
Axes of the slice: x: 2, y: 2, z: 4, core: 2. Of those that a mesh axis runs over, the one named last changes fastest.
Arguments:
- hidden_states: bfloat16 [512, 3584], P('seq', 'vocab'), may hold values from -6 to 6
- norm_gain: float32 [3584], replicated, may hold values from 0.5 to 1.5
- embedding: bfloat16 [256000, 3584], P(('vocab', 'seq')), may hold values from -0.29882812 to 0.29882812
- targets: int32 [512], replicated, may hold values from 0 to 255999
Outputs:
- token_loss: float32 [512], P('seq')
- mean_loss: float32 [], replicated
All inputs are finite; a program needn't handle non-finite values.
Results may differ from a plain program's by a relative error of at most 0.0005.
Values may be sent and summed in bfloat16 or wider, within the bound.
A program may use at most 128 MiB of HBM per device.

v0:
```python
import jax
import jax.numpy as jnp
from jax import lax
from jax.sharding import PartitionSpec as P


def normalize(rows, norm_gain):
    values = rows.astype(jnp.float32)
    meansq = jnp.mean(values * values, axis=-1, keepdims=True)
    return (values * lax.rsqrt(meansq + 1e-06) * norm_gain).astype(jnp.bfloat16)


def vocab_terms_of(embedding, targets, normed_rows):
    local_rows = embedding.shape[0]
    base = (lax.axis_index("vocab") * lax.axis_size("seq") + lax.axis_index("seq")) * local_rows
    scores = jnp.einsum("vd,td->vt", embedding, normed_rows, preferred_element_type=jnp.float32)
    capped = 30.0 * jnp.tanh(scores / 30.0)
    total = jnp.sum(jnp.exp(capped), axis=0)
    ids = base + jnp.arange(local_rows, dtype=jnp.int32)
    hit = ids[:, None] == targets[None, :]
    picked = jnp.sum(jnp.where(hit, capped, 0.0), axis=0)
    return (total, picked)


def local(hidden_states, norm_gain, embedding, targets):
    own_count = hidden_states.shape[0]
    all_count = targets.shape[0]
    gathered_rows = lax.all_gather(hidden_states, "seq", axis=0, tiled=True)
    whole = lax.all_gather(gathered_rows, "vocab", axis=1, tiled=True)
    normed = normalize(whole, norm_gain)
    total, picked = vocab_terms_of(embedding, targets, normed)
    total, picked = lax.psum((total, picked), ("vocab", "seq"))
    every_loss = jnp.log(total) - picked
    mean_loss = jnp.sum(every_loss) / all_count
    token_loss = lax.dynamic_slice_in_dim(every_loss, lax.axis_index("seq") * own_count, own_count)
    return (token_loss, mean_loss)


def solution(mesh):
    placed = (P("seq", "vocab"), P(), P(("vocab", "seq"), None), P())
    return jax.shard_map(
        local, mesh=mesh, in_specs=placed, out_specs=(P("seq"), P()), check_vma=False
    )
```

profile of v0, /device:TPU:0, one launch (start us, length us, event | category | flops | bytes accessed | tf_op | source)
XLA Modules:
  0.0 157.3 jit_solution(12015956932428505481)
XLA Ops:
  7.2 0.0 all-gather.2.cloned.1.call-start
  7.2 8.7 %all_gather.6 = bf16[512,224]{0,1:T(8,128)(2,1)} all-gather(bf16[256,224]{0,1:T(8,128)(2,1)} %param.4), channel_id=1, replica_groups=mesh['vocab'=16,'seq'=2] {'seq'}, dimensions={0}, use_global_device_ids=true | all-gather | bytes 344064 | tf_op jit(solution)/shard_map/all_gather | solution.py:28
  15.9 0.0 all-gather.2.cloned.1.call-update
  15.9 48.1 %all-gather.2.cloned.1.call-done = bf16[512,3584]{0,1:T(8,128)(2,1)} async-done(((bf16[512,224]{0,1:T(8,128)(2,1)}), bf16[512,3584]{0,1:T(8,128)(2,1)}) %all-gather.2.cloned.1.call-update) | async-done | bytes 3670032 | tf_op jit(solution)/shard_map/all_gather | solution.py:29
  64.0 2.9 %fusion.2 = f32[512]{0:T(512)S(1)} fusion(bf16[512,3584]{0,1:T(8,128)(2,1)} %all-gather.2.cloned.1.call-done), kind=kLoop, calls=%fused_computation.7 | loop fusion | flops 5504512 | bytes 3672064 | tf_op jit(solution)/shard_map/reduce_sum | solution.py:9
  66.9 41.1 %fusion = (f32[512]{0:T(512)S(1)}, f32[512]{0:T(512)S(1)}) fusion(s32[512]{0:T(512)} %param.7, s32[8000]{0:T(1024)S(1)} %iota_add_fusion, bf16[8000,3584]{1,0:T(8,128)(2,1)} %param.6, bf16[512,3584]{0,1:T(8,128)(2,1)} %all-gather.2.cloned.1.call-done, f32[3584]{0:T(1024)} %param.5, f32[512]{0:T(512)S(1)} %add_rsqrt_fusion), kind=kOutput, calls=%fused_computation.2 | convolution fusion | flops 29392044032 | bytes 61068544 | tf_op jit(solution)/shard_map/vd,td->vt/dot_general | solution.py:16
  108.0 39.4 %all-reduce = (f32[512]{0:T(512)S(1)}, f32[512]{0:T(512)S(1)}) all-reduce(f32[512]{0:T(512)S(1)} %get-tuple-element.3, f32[512]{0:T(512)S(1)} %get-tuple-element.2), channel_id=1, replica_groups=mesh['vocab'=16,'seq'=2] {'vocab','seq'}, use_global_device_ids=true, to_apply=%region_4.5 | all-reduce | flops 1024 | bytes 8192 | tf_op jit(solution)/shard_map/psum | solution.py:32
  147.4 0.6 fusion.8
  148.7 0.6 dynamic_slice.3
  (2 shorter events, 0.0 us)
Async XLA Ops:
  7.2 56.8 %all-gather.2.cloned.1.call-start = ((), (), s32[]{:S(2)}) async-start(), calls=%async_computation | async-start | bytes 3899392 | tf_op jit(solution)/shard_map/all_gather | solution.py:29
Sparse Core Ops, SparseCore 0:
  16.0 47.9 all-gather.1
where the time goes:
time: 158 us; the launch traced here: 157 us
  blocking collectives  48.1 us (30%)
  waiting for transfers between devices  48.1 us (30%)
  matrix products  41.1 us (26%)
  between operations  15.8 us (10%)
  other arithmetic  3.5 us (2%)
    all_gather x1, waiting for transfers between devices, local(): whole = lax.all_gather(gathered_rows, 'vocab', axis=1, tiled=True)  48.1 us
    dot_general x1, matrix products, vocab_terms_of(): jnp.einsum('vd,td->vt', embedding, normed_rows, preferred_element_type=jn...  41.1 us
    psum x1, blocking collectives, local(): total, picked = lax.psum((total, picked), ('vocab', 'seq'))  39.4 us
    all_gather x1, blocking collectives, local(): gathered_rows = lax.all_gather(hidden_states, 'seq', axis=0, tiled=True)  8.67 us
  transfers between devices with their start and end apart: 1, of which 1 were waited for; matrix products, arithmetic and copies ran while one was open for 0% of the time, Pallas kernels for 0%

commit v1 on v0

--- a/solution.py
+++ b/solution.py
@@ -29,7 +29,7 @@
     whole = lax.all_gather(gathered_rows, "vocab", axis=1, tiled=True)
     normed = normalize(whole, norm_gain)
     total, picked = vocab_terms_of(embedding, targets, normed)
-    total, picked = lax.psum((total, picked), ("vocab", "seq"))
+    total, picked = lax.psum(lax.psum((total, picked), "seq"), "vocab")
     every_loss = jnp.log(total) - picked
     mean_loss = jnp.sum(every_loss) / all_count
     token_loss = lax.dynamic_slice_in_dim(every_loss, lax.axis_index("seq") * own_count, own_count)

time: 158 us -> 153 us (0.968)
  blocking collectives: 48.1 us -> 43.8 us
    psum x1 -> x2, blocking collectives: 39.4 us -> 35.1 us  [local(): total, picked = lax.psum(lax.psum((total, picked), 'seq'), 'vocab')]
where the time goes in v1:
time: 153 us
  waiting for transfers between devices  48.1 us (31%)
  blocking collectives  43.8 us (29%)
  matrix products  41.1 us (27%)
  between operations  15.8 us (10%)
  other arithmetic  3.5 us (2%)
    all_gather x1, waiting for transfers between devices, local(): whole = lax.all_gather(gathered_rows, 'vocab', axis=1, tiled=True)  48.1 us
    dot_general x1, matrix products, vocab_terms_of(): jnp.einsum('vd,td->vt', embedding, normed_rows, preferred_element_type=jn...  41.1 us
    psum x2, blocking collectives, local(): total, picked = lax.psum(lax.psum((total, picked), 'seq'), 'vocab')  35.1 us
    all_gather x1, blocking collectives, local(): gathered_rows = lax.all_gather(hidden_states, 'seq', axis=0, tiled=True)  8.67 us
  transfers between devices with their start and end apart: 1, of which 1 were waited for; matrix products, arithmetic and copies ran while one was open for 0% of the time, Pallas kernels for 0%

profile of v1, /device:TPU:0, one launch (start us, length us, event | category | flops | bytes accessed | tf_op | source)
XLA Modules:
  0.0 153.0 jit_solution(10168680514422203857)
XLA Ops:
  7.2 0.0 all-gather.2.cloned.1.call-start
  7.2 8.7 %all_gather.6 = bf16[512,224]{0,1:T(8,128)(2,1)} all-gather(bf16[256,224]{0,1:T(8,128)(2,1)} %param.4), channel_id=1, replica_groups=mesh['vocab'=16,'seq'=2] {'seq'}, dimensions={0}, use_global_device_ids=true | all-gather | bytes 344064 | tf_op jit(solution)/shard_map/all_gather | solution.py:28
  15.9 0.0 all-gather.2.cloned.1.call-update
  15.9 48.1 %all-gather.2.cloned.1.call-done = bf16[512,3584]{0,1:T(8,128)(2,1)} async-done(((bf16[512,224]{0,1:T(8,128)(2,1)}), bf16[512,3584]{0,1:T(8,128)(2,1)}) %all-gather.2.cloned.1.call-update) | async-done | bytes 3670032 | tf_op jit(solution)/shard_map/all_gather | solution.py:29
  64.0 2.9 %fusion.2 = f32[512]{0:T(512)S(1)} fusion(bf16[512,3584]{0,1:T(8,128)(2,1)} %all-gather.2.cloned.1.call-done), kind=kLoop, calls=%fused_computation.7 | loop fusion | flops 5504512 | bytes 3672064 | tf_op jit(solution)/shard_map/reduce_sum | solution.py:9
  66.9 41.1 %fusion = (f32[512]{0:T(512)S(1)}, f32[512]{0:T(512)S(1)}) fusion(s32[512]{0:T(512)} %param.7, s32[8000]{0:T(1024)S(1)} %iota_add_fusion, bf16[8000,3584]{1,0:T(8,128)(2,1)} %param.6, bf16[512,3584]{0,1:T(8,128)(2,1)} %all-gather.2.cloned.1.call-done, f32[3584]{0:T(1024)} %param.5, f32[512]{0:T(512)S(1)} %add_rsqrt_fusion), kind=kOutput, calls=%fused_computation.2 | convolution fusion | flops 29392044032 | bytes 61068544 | tf_op jit(solution)/shard_map/vd,td->vt/dot_general | solution.py:16
  108.0 4.9 %all-reduce.1 = (f32[512]{0:T(512)S(1)}, f32[512]{0:T(512)S(1)}) all-reduce(f32[512]{0:T(512)S(1)} %get-tuple-element.3, f32[512]{0:T(512)S(1)} %get-tuple-element.2), channel_id=1, replica_groups=mesh['vocab'=16,'seq'=2] {'seq'}, use_global_device_ids=true, to_apply=%region_5.6 | all-reduce | flops 1024 | bytes 8192 | tf_op jit(solution)/shard_map/psum | solution.py:32
  113.0 30.2 %all-reduce = (f32[512]{0:T(512)S(1)}, f32[512]{0:T(512)S(1)}) all-reduce(f32[512]{0:T(512)S(1)} %get-tuple-element.6, f32[512]{0:T(512)S(1)} %get-tuple-element.7), channel_id=1, replica_groups=mesh['vocab'=16,'seq'=2] {'vocab'}, use_global_device_ids=true, to_apply=%region_6.7 | all-reduce | flops 1024 | bytes 8192 | tf_op jit(solution)/shard_map/psum | solution.py:32
  143.1 0.6 fusion.8
  144.4 0.6 dynamic_slice.3
  (2 shorter events, 0.0 us)
Async XLA Ops:
  7.2 56.8 %all-gather.2.cloned.1.call-start = ((), (), s32[]{:S(2)}) async-start(), calls=%async_computation | async-start | bytes 3899392 | tf_op jit(solution)/shard_map/all_gather | solution.py:29
Sparse Core Ops, SparseCore 0:
  16.0 47.9 all-gather.1
